TPU v7x, 32 devices: a whole 2x2x4 slice. The times are simulated.
32 devices in a mesh: grp: 4 (over z), seq: 8 (over y, x, core).
Axes of the slice: x: 2, y: 2, z: 4, core: 2. Of those that a mesh axis runs over, the one named last changes fastest.
Arguments:
- inputs: bfloat16 [8192, 1024], P(('grp', 'seq')), may hold values from -12 to 12
- noise: bfloat16 [8192, 1024], P(('grp', 'seq')), may hold values from -6 to 6
- cotangent: bfloat16 [8192, 1024], P(('grp', 'seq')), may hold values from -12 to 12
- lengths: int32 [4, 3], P('grp'), may hold values from 400 to 1024, as said below
- span_starts: int32 [4, 20], P('grp'), may hold values from 0 to 2038
- ffn1_gain: bfloat16 [1024], P('seq'), may hold values from 0.099609375 to 1.8984375
- ffn1_up: bfloat16 [1024, 4096], P('seq'), may hold values from -0.1875 to 0.1875
- ffn1_down: bfloat16 [4096, 1024], P('seq'), may hold values from -0.09375 to 0.09375
- att_gain: bfloat16 [1024], P('seq'), may hold values from 0.099609375 to 1.8984375
- qkv_weight: bfloat16 [1024, 3072], P('seq'), may hold values from -0.1875 to 0.1875
- out_weight: bfloat16 [1024, 1024], P('seq'), may hold values from -0.75 to 0.75
- rel_bias: bfloat16 [8, 32], P('seq'), may hold values from -4 to 4
- conv_gain: bfloat16 [1024], P('seq'), may hold values from 0.099609375 to 1.8984375
- point1_weight: bfloat16 [1024, 2048], P('seq'), may hold values from -0.1875 to 0.1875
- depth_weight: bfloat16 [5, 1024], P(None, 'seq'), may hold values from -2.5 to 2.5
- bn_gain: bfloat16 [1024], P('seq'), may hold values from 0.099609375 to 1.8984375
- bn_shift: bfloat16 [1024], P('seq'), may hold values from -3 to 3
- point2_weight: bfloat16 [1024, 1024], P('seq'), may hold values from -0.1875 to 0.1875
- ffn2_gain: bfloat16 [1024], P('seq'), may hold values from 0.099609375 to 1.8984375
- ffn2_up: bfloat16 [1024, 4096], P('seq'), may hold values from -0.1875 to 0.1875
- ffn2_down: bfloat16 [4096, 1024], P('seq'), may hold values from -0.09375 to 0.09375
- final_gain: bfloat16 [1024], P('seq'), may hold values from 0.099609375 to 1.8984375
Outputs:
- output: bfloat16 [8192, 1024], P(('grp', 'seq'))
- input_grad: bfloat16 [8192, 1024], P(('grp', 'seq'))
- ffn1_gain_grad: float32 [1024], P('seq')
- ffn1_up_grad: float32 [1024, 4096], P('seq')
- ffn1_down_grad: float32 [4096, 1024], P('seq')
- att_gain_grad: float32 [1024], P('seq')
- qkv_weight_grad: float32 [1024, 3072], P('seq')
- out_weight_grad: float32 [1024, 1024], P('seq')
- rel_bias_grad: float32 [8, 32], P('seq')
- conv_gain_grad: float32 [1024], P('seq')
- point1_weight_grad: float32 [1024, 2048], P('seq')
- depth_weight_grad: float32 [5, 1024], P(None, 'seq')
- bn_gain_grad: float32 [1024], P('seq')
- bn_shift_grad: float32 [1024], P('seq')
- point2_weight_grad: float32 [1024, 1024], P('seq')
- ffn2_gain_grad: float32 [1024], P('seq')
- ffn2_up_grad: float32 [1024, 4096], P('seq')
- ffn2_down_grad: float32 [4096, 1024], P('seq')
- final_gain_grad: float32 [1024], P('seq')
Inputs may be any that keep to these rules, and one draw needn't show every extreme that they name: Each row holds 3 lengths that sum to 2048; each is at least 400, and exactly one in every row is 1024. `span_starts`: spans may intersect one another and utterance ends.
All inputs are finite; a program needn't handle non-finite values.
Results may differ from a plain program's by a relative error of at most 0.02.
Values may be sent and summed in bfloat16 or wider, within the bound.
A program may use at most 256 MiB of HBM per device.

v0:
```python
import jax
import jax.numpy as jnp
from jax import lax
from jax.sharding import PartitionSpec as P

KERNEL = 5
SPAN_LEN = 10
HEAD_DIM = 128


epsilon = 1e-05
limits = (8, 16, 32, 64, 128, 256, 512, 1024)
highest = lax.Precision.HIGHEST


def extended(block, sides, width):
    for axis, dim in sides:
        count = lax.axis_size(axis)
        forward = [(i, i + 1) for i in range(count - 1)]
        backward = [(target, source) for source, target in forward]
        low = lax.ppermute(
            lax.slice_in_dim(block, block.shape[dim] - width, None, axis=dim), axis, forward
        )
        high = lax.ppermute(lax.slice_in_dim(block, 0, width, axis=dim), axis, backward)
        block = jnp.concatenate([low, block, high], axis=dim)
    return block


def bucket_of(distance):
    magnitude = jnp.abs(distance)
    result = jnp.minimum(magnitude, 7)
    for bound_at in limits:
        result = result + (magnitude >= bound_at).astype(jnp.int32)
    return result + 16 * (distance > 0).astype(jnp.int32)


def normalize(tensor, gain_vec):
    centred = tensor - jnp.mean(tensor, axis=-1, keepdims=True)
    factor = lax.rsqrt(jnp.mean(centred * centred, axis=-1, keepdims=True) + epsilon)
    normed = centred * factor
    return (normed * gain_vec, normed, factor)


def normalize_back(grad_out, normed, factor, gain_vec):
    grad_gain = jnp.sum(grad_out * normed, axis=0)
    scaled = grad_out * gain_vec
    grad_in = factor * (
        scaled
        - jnp.mean(scaled, axis=-1, keepdims=True)
        - normed * jnp.mean(scaled * normed, axis=-1, keepdims=True)
    )
    return (grad_in, grad_gain)


def matmul(left, right):
    return jnp.dot(left, right, preferred_element_type=jnp.float32)


def left_product(left, right):
    return lax.dot_general(
        left, right, (((0,), (0,)), ((), ())), preferred_element_type=jnp.float32
    )


def right_product(left, right):
    return lax.dot_general(
        left, right, (((1,), (1,)), ((), ())), preferred_element_type=jnp.float32
    )


def swish_slope(pre_act):
    sig_val = jax.nn.sigmoid(pre_act)
    return sig_val * (1.0 + pre_act * (1.0 - sig_val))


def ffn_forward(hidden, gain_vec, up_proj, down_proj):
    normal_out, normed, factor = normalize(hidden, gain_vec)
    act_low = normal_out.astype(jnp.bfloat16)
    pre_act = matmul(act_low, up_proj)
    inner_low = jax.nn.silu(pre_act).astype(jnp.bfloat16)
    result = hidden + 0.5 * matmul(inner_low, down_proj)
    return (result, (act_low, pre_act, inner_low, normed, factor))


def ffn_backward(grad_h, saved_ffn, gain_vec, up_proj, down_proj):
    act_low, pre_act, inner_low, normed, factor = saved_ffn
    grad_branch = (0.5 * grad_h).astype(jnp.bfloat16)
    grad_down = left_product(inner_low, grad_branch)
    grad_pre = (right_product(grad_branch, down_proj) * swish_slope(pre_act)).astype(jnp.bfloat16)
    grad_up = left_product(act_low, grad_pre)
    grad_in, grad_gain = normalize_back(right_product(grad_pre, up_proj), normed, factor, gain_vec)
    return (grad_h + grad_in, grad_gain, grad_up, grad_down)


def relative_bias(table, first_row, block_len, group_len):
    heads_here = table.shape[0]
    span_len = group_len + block_len - 1
    distance = jnp.arange(span_len, dtype=jnp.int32) - (block_len - 1) - first_row
    onehot = (
        bucket_of(distance)[:, None] == jnp.arange(table.shape[1], dtype=jnp.int32)[None, :]
    ).astype(jnp.float32)
    bias_line = jnp.dot(table, onehot.T, precision=highest)
    bias_line = jnp.concatenate([bias_line, jnp.zeros((heads_here, 1), jnp.float32)], axis=1)
    bias_tiles = jnp.broadcast_to(
        bias_line[:, None, :], (heads_here, block_len, span_len + 1)
    ).reshape(heads_here, -1)
    bias_tiles = bias_tiles[:, : block_len * span_len].reshape(heads_here, block_len, span_len)
    return (bias_tiles[:, :, block_len - 1 : block_len - 1 + group_len], onehot)


def diagonal_sums(grad_block, block_len, group_len):
    heads_here = grad_block.shape[0]
    span_len = group_len + block_len - 1
    padded = jnp.pad(grad_block, ((0, 0), (0, 0), (block_len - 1, 0)))
    flat_grads = jnp.pad(padded.reshape(heads_here, block_len * span_len), ((0, 0), (0, block_len)))
    return jnp.sum(flat_grads.reshape(heads_here, block_len, span_len + 1), axis=1)[:, :span_len]


def block_scores(query_b, keys_all, segment, table, first_row):
    block_len = query_b.shape[0]
    group_len = keys_all.shape[0]
    scaling = query_b.shape[-1] ** (-0.5)
    bias_mat, onehot = relative_bias(table, first_row, block_len, group_len)
    raw_scores = (
        jnp.einsum("qhd,khd->hqk", query_b, keys_all, preferred_element_type=jnp.float32) * scaling
        + bias_mat
    )
    seg_rows = lax.dynamic_slice_in_dim(segment, first_row, block_len, 0)
    same_utt = (seg_rows[:, None] == segment[None, :])[None]
    return (jnp.where(same_utt, raw_scores, -1e30), onehot)


def per_device(
    inputs,
    noise,
    cotangent,
    lengths,
    span_starts,
    ffn1_gain,
    ffn1_up,
    ffn1_down,
    att_gain,
    qkv_weight,
    out_weight,
    rel_bias,
    conv_gain,
    point1_weight,
    depth_weight,
    bn_gain,
    bn_shift,
    point2_weight,
    ffn2_gain,
    ffn2_up,
    ffn2_down,
    final_gain,
):
    frame_count = inputs.shape[0]
    model_width = inputs.shape[1]
    group_len = frame_count * lax.axis_size("seq")
    total_len = group_len * lax.axis_size("grp")
    offset = lax.axis_index("seq") * frame_count
    block_len = min(512, group_len)
    block_count = group_len // block_len
    (
        gain_ffn1,
        up_one,
        down_one,
        gain_att,
        w_qkv,
        w_out,
        gain_conv,
        w_point1,
        w_depth,
        gain_bn,
        shift_bn,
        w_point2,
        gain_ffn2,
        up_two,
        down_two,
        gain_final,
    ) = (
        lax.all_gather(ffn1_gain, "seq", axis=0, tiled=True),
        lax.all_gather(ffn1_up, "seq", axis=0, tiled=True),
        lax.all_gather(ffn1_down, "seq", axis=0, tiled=True),
        lax.all_gather(att_gain, "seq", axis=0, tiled=True),
        lax.all_gather(qkv_weight, "seq", axis=0, tiled=True),
        lax.all_gather(out_weight, "seq", axis=0, tiled=True),
        lax.all_gather(conv_gain, "seq", axis=0, tiled=True),
        lax.all_gather(point1_weight, "seq", axis=0, tiled=True),
        lax.all_gather(depth_weight, "seq", axis=1, tiled=True),
        lax.all_gather(bn_gain, "seq", axis=0, tiled=True),
        lax.all_gather(bn_shift, "seq", axis=0, tiled=True),
        lax.all_gather(point2_weight, "seq", axis=0, tiled=True),
        lax.all_gather(ffn2_gain, "seq", axis=0, tiled=True),
        lax.all_gather(ffn2_up, "seq", axis=0, tiled=True),
        lax.all_gather(ffn2_down, "seq", axis=0, tiled=True),
        lax.all_gather(final_gain, "seq", axis=0, tiled=True),
    )
    utt_ends = jnp.cumsum(lengths[0])
    places = jnp.arange(group_len, dtype=jnp.int32)
    segment = jnp.sum((places[:, None] >= utt_ends[None, :]).astype(jnp.int32), axis=1)
    local_at = offset + jnp.arange(frame_count, dtype=jnp.int32)
    begins = span_starts[0]
    covered = jnp.any(
        (local_at[:, None] >= begins[None, :]) & (local_at[:, None] < begins[None, :] + SPAN_LEN),
        axis=1,
    )
    hidden_zero = jnp.where(covered[:, None], noise.astype(jnp.float32), inputs.astype(jnp.float32))
    hidden_one, saved_one = ffn_forward(hidden_zero, gain_ffn1, up_one, down_one)
    att_out, att_normed, att_factor = normalize(hidden_one, gain_att)
    att_low = att_out.astype(jnp.bfloat16)
    qkv_low = matmul(att_low, w_qkv).astype(jnp.bfloat16).reshape(frame_count, 3, model_width)
    by_head = lax.all_to_all(qkv_low, "seq", split_axis=2, concat_axis=0, tiled=True)
    heads_here = by_head.shape[2] // HEAD_DIM
    queries = by_head[:, 0].reshape(group_len, heads_here, HEAD_DIM)
    keys_all = by_head[:, 1].reshape(group_len, heads_here, HEAD_DIM)
    values_all = by_head[:, 2].reshape(group_len, heads_here, HEAD_DIM)
    table = rel_bias.astype(jnp.float32)

    def forward_block(block_idx):
        first_row = block_idx * block_len
        query_b = lax.dynamic_slice_in_dim(queries, first_row, block_len, 0)
        scores, onehot = block_scores(query_b, keys_all, segment, table, first_row)
        row_peak = jnp.max(scores, axis=-1, keepdims=True)
        shifted = jnp.exp(scores - row_peak)
        row_total = jnp.sum(shifted, axis=-1, keepdims=True)
        prob_low = (shifted / row_total).astype(jnp.bfloat16)
        block_out = jnp.einsum(
            "hqk,khd->qhd", prob_low, values_all, preferred_element_type=jnp.float32
        )
        return (block_out, (row_peak + jnp.log(row_total))[..., 0])

    out_blocks, lse_blocks = lax.map(forward_block, jnp.arange(block_count, dtype=jnp.int32))
    attended = out_blocks.reshape(group_len, heads_here * HEAD_DIM).astype(jnp.bfloat16)
    back_time = lax.all_to_all(attended, "seq", split_axis=0, concat_axis=1, tiled=True)
    hidden_two = hidden_one + matmul(back_time, w_out)
    conv_out, conv_normed, conv_factor = normalize(hidden_two, gain_conv)
    conv_low = conv_out.astype(jnp.bfloat16)
    gated = matmul(conv_low, w_point1)
    linear_part = gated[:, :model_width]
    sig_gate = jax.nn.sigmoid(gated[:, model_width:])
    glu_low = (linear_part * sig_gate).astype(jnp.bfloat16)
    glu_rim = extended(glu_low, (("seq", 0),), 2)
    seg_window = lax.dynamic_slice_in_dim(
        jnp.pad(segment, 2, constant_values=-1), offset, frame_count + 4, 0
    )
    centre_seg = seg_window[2 : 2 + frame_count]
    tap_weights = w_depth.astype(jnp.float32)
    conv_sum = jnp.zeros((frame_count, model_width), jnp.float32)
    for tap_at in range(KERNEL):
        same_utt = (seg_window[tap_at : tap_at + frame_count] == centre_seg)[:, None]
        conv_sum = conv_sum + tap_weights[tap_at] * jnp.where(
            same_utt, glu_rim[tap_at : tap_at + frame_count].astype(jnp.float32), 0.0
        )
    mean_c = lax.psum(jnp.sum(conv_sum, axis=0), ("grp", "seq")) / total_len
    centred = conv_sum - mean_c
    var_c = lax.psum(jnp.sum(centred * centred, axis=0), ("grp", "seq")) / total_len
    inv_std = lax.rsqrt(var_c + epsilon)
    normed_bn = centred * inv_std
    bn_value = normed_bn * gain_bn + shift_bn
    swish_low = jax.nn.silu(bn_value).astype(jnp.bfloat16)
    hidden_three = hidden_two + matmul(swish_low, w_point2)
    hidden_four, saved_two = ffn_forward(hidden_three, gain_ffn2, up_two, down_two)
    final_out, final_normed, final_factor = normalize(hidden_four, gain_final)
    output = final_out.astype(jnp.bfloat16)
    (
        gain_ffn1,
        up_one,
        down_one,
        gain_att,
        w_qkv,
        w_out,
        gain_conv,
        w_point1,
        w_depth,
        gain_bn,
        shift_bn,
        w_point2,
        gain_ffn2,
        up_two,
        down_two,
        gain_final,
    ) = (
        lax.all_gather(ffn1_gain, "seq", axis=0, tiled=True),
        lax.all_gather(ffn1_up, "seq", axis=0, tiled=True),
        lax.all_gather(ffn1_down, "seq", axis=0, tiled=True),
        lax.all_gather(att_gain, "seq", axis=0, tiled=True),
        lax.all_gather(qkv_weight, "seq", axis=0, tiled=True),
        lax.all_gather(out_weight, "seq", axis=0, tiled=True),
        lax.all_gather(conv_gain, "seq", axis=0, tiled=True),
        lax.all_gather(point1_weight, "seq", axis=0, tiled=True),
        lax.all_gather(depth_weight, "seq", axis=1, tiled=True),
        lax.all_gather(bn_gain, "seq", axis=0, tiled=True),
        lax.all_gather(bn_shift, "seq", axis=0, tiled=True),
        lax.all_gather(point2_weight, "seq", axis=0, tiled=True),
        lax.all_gather(ffn2_gain, "seq", axis=0, tiled=True),
        lax.all_gather(ffn2_up, "seq", axis=0, tiled=True),
        lax.all_gather(ffn2_down, "seq", axis=0, tiled=True),
        lax.all_gather(final_gain, "seq", axis=0, tiled=True),
    )
    tap_weights = w_depth.astype(jnp.float32)
    grad_four, grad_gfinal = normalize_back(
        cotangent.astype(jnp.float32), final_normed, final_factor, gain_final
    )
    grad_three, grad_gffn2, grad_up2, grad_down2 = ffn_backward(
        grad_four, saved_two, gain_ffn2, up_two, down_two
    )
    grad_branch = grad_three.astype(jnp.bfloat16)
    grad_point2 = left_product(swish_low, grad_branch)
    grad_bn = right_product(grad_branch, w_point2) * swish_slope(bn_value)
    grad_gain_bn = jnp.sum(grad_bn * normed_bn, axis=0)
    grad_shift_bn = jnp.sum(grad_bn, axis=0)
    grad_normed = grad_bn * gain_bn
    sum_plain, sum_cross = lax.psum(
        (jnp.sum(grad_normed, axis=0), jnp.sum(grad_normed * normed_bn, axis=0)), ("grp", "seq")
    )
    grad_conv = (
        inv_std * (grad_normed - sum_plain / total_len - normed_bn * (sum_cross / total_len))
    ).astype(jnp.bfloat16)
    grad_rim = extended(grad_conv, (("seq", 0),), 2)
    grad_glu = jnp.zeros((frame_count, model_width), jnp.float32)
    tap_grads = []
    for tap_at in range(KERNEL):
        same_fwd = (seg_window[tap_at : tap_at + frame_count] == centre_seg)[:, None]
        tap_grads.append(
            jnp.sum(
                jnp.where(
                    same_fwd,
                    grad_conv.astype(jnp.float32)
                    * glu_rim[tap_at : tap_at + frame_count].astype(jnp.float32),
                    0.0,
                ),
                axis=0,
            )
        )
        mirror = KERNEL - 1 - tap_at
        same_back = (seg_window[mirror : mirror + frame_count] == centre_seg)[:, None]
        grad_glu = grad_glu + tap_weights[tap_at] * jnp.where(
            same_back, grad_rim[mirror : mirror + frame_count].astype(jnp.float32), 0.0
        )
    grad_depth = jnp.stack(tap_grads)
    grad_gated = jnp.concatenate(
        [grad_glu * sig_gate, grad_glu * linear_part * sig_gate * (1.0 - sig_gate)], axis=1
    ).astype(jnp.bfloat16)
    grad_point1 = left_product(conv_low, grad_gated)
    grad_in3, grad_gconv = normalize_back(
        right_product(grad_gated, w_point1), conv_normed, conv_factor, gain_conv
    )
    grad_two = grad_three + grad_in3
    grad_att = grad_two.astype(jnp.bfloat16)
    grad_wout = left_product(back_time, grad_att)
    grad_attended = right_product(grad_att, w_out).astype(jnp.bfloat16)
    grad_heads = lax.all_to_all(
        grad_attended, "seq", split_axis=1, concat_axis=0, tiled=True
    ).reshape(group_len, heads_here, HEAD_DIM)

    def backward_block(carried, scan_item):
        grad_keys, grad_values, grad_table = carried
        block_idx, lse_b = scan_item
        first_row = block_idx * block_len
        query_b = lax.dynamic_slice_in_dim(queries, first_row, block_len, 0)
        grad_b = lax.dynamic_slice_in_dim(grad_heads, first_row, block_len, 0)
        scores, onehot = block_scores(query_b, keys_all, segment, table, first_row)
        prob_vals = jnp.exp(scores - lse_b[..., None])
        prob_low = prob_vals.astype(jnp.bfloat16)
        grad_values = grad_values + jnp.einsum(
            "hqk,qhd->khd", prob_low, grad_b, preferred_element_type=jnp.float32
        )
        grad_probs = jnp.einsum(
            "qhd,khd->hqk", grad_b, values_all, preferred_element_type=jnp.float32
        )
        row_term = jnp.sum(prob_vals * grad_probs, axis=-1, keepdims=True)
        grad_scores = (prob_vals * (grad_probs - row_term)).astype(jnp.bfloat16)
        scaling = HEAD_DIM ** (-0.5)
        grad_query = (
            jnp.einsum("hqk,khd->qhd", grad_scores, keys_all, preferred_element_type=jnp.float32)
            * scaling
        )
        grad_keys = (
            grad_keys
            + jnp.einsum("hqk,qhd->khd", grad_scores, query_b, preferred_element_type=jnp.float32)
            * scaling
        )
        grad_table = grad_table + jnp.dot(
            diagonal_sums(grad_scores.astype(jnp.float32), block_len, group_len),
            onehot,
            precision=highest,
        )
        return ((grad_keys, grad_values, grad_table), grad_query)

    zero_heads = jnp.zeros((group_len, heads_here, HEAD_DIM), jnp.float32)
    (grad_keys, grad_values, grad_table), query_blocks = lax.scan(
        backward_block,
        (zero_heads, zero_heads, jnp.zeros(table.shape, jnp.float32)),
        (jnp.arange(block_count, dtype=jnp.int32), lse_blocks),
    )
    grad_query = query_blocks.reshape(group_len, heads_here, HEAD_DIM)
    stacked = (
        jnp.stack([grad_query, grad_keys, grad_values], axis=1)
        .reshape(group_len, 3, heads_here * HEAD_DIM)
        .astype(jnp.bfloat16)
    )
    grad_qkv = lax.all_to_all(stacked, "seq", split_axis=0, concat_axis=2, tiled=True).reshape(
        frame_count, 3 * model_width
    )
    grad_wqkv = left_product(att_low, grad_qkv)
    grad_in2, grad_gatt = normalize_back(
        right_product(grad_qkv, w_qkv), att_normed, att_factor, gain_att
    )
    grad_one = grad_two + grad_in2
    grad_zero, grad_gffn1, grad_up1, grad_down1 = ffn_backward(
        grad_one, saved_one, gain_ffn1, up_one, down_one
    )
    input_grad = jnp.where(covered[:, None], 0.0, grad_zero).astype(jnp.bfloat16)
    shard_grads = (
        lax.psum_scatter(
            grad_gffn1.astype(jnp.bfloat16), "seq", scatter_dimension=0, tiled=True
        ).astype(jnp.float32),
        lax.psum_scatter(
            grad_up1.astype(jnp.bfloat16), "seq", scatter_dimension=0, tiled=True
        ).astype(jnp.float32),
        lax.psum_scatter(
            grad_down1.astype(jnp.bfloat16), "seq", scatter_dimension=0, tiled=True
        ).astype(jnp.float32),
        lax.psum_scatter(
            grad_gatt.astype(jnp.bfloat16), "seq", scatter_dimension=0, tiled=True
        ).astype(jnp.float32),
        lax.psum_scatter(
            grad_wqkv.astype(jnp.bfloat16), "seq", scatter_dimension=0, tiled=True
        ).astype(jnp.float32),
        lax.psum_scatter(
            grad_wout.astype(jnp.bfloat16), "seq", scatter_dimension=0, tiled=True
        ).astype(jnp.float32),
        lax.psum_scatter(
            grad_gconv.astype(jnp.bfloat16), "seq", scatter_dimension=0, tiled=True
        ).astype(jnp.float32),
        lax.psum_scatter(
            grad_point1.astype(jnp.bfloat16), "seq", scatter_dimension=0, tiled=True
        ).astype(jnp.float32),
        lax.psum_scatter(
            grad_depth.astype(jnp.bfloat16), "seq", scatter_dimension=1, tiled=True
        ).astype(jnp.float32),
        lax.psum_scatter(
            grad_gain_bn.astype(jnp.bfloat16), "seq", scatter_dimension=0, tiled=True
        ).astype(jnp.float32),
        lax.psum_scatter(
            grad_shift_bn.astype(jnp.bfloat16), "seq", scatter_dimension=0, tiled=True
        ).astype(jnp.float32),
        lax.psum_scatter(
            grad_point2.astype(jnp.bfloat16), "seq", scatter_dimension=0, tiled=True
        ).astype(jnp.float32),
        lax.psum_scatter(
            grad_gffn2.astype(jnp.bfloat16), "seq", scatter_dimension=0, tiled=True
        ).astype(jnp.float32),
        lax.psum_scatter(
            grad_up2.astype(jnp.bfloat16), "seq", scatter_dimension=0, tiled=True
        ).astype(jnp.float32),
        lax.psum_scatter(
            grad_down2.astype(jnp.bfloat16), "seq", scatter_dimension=0, tiled=True
        ).astype(jnp.float32),
        lax.psum_scatter(
            grad_gfinal.astype(jnp.bfloat16), "seq", scatter_dimension=0, tiled=True
        ).astype(jnp.float32),
    )
    (
        sum_gffn1,
        sum_up1,
        sum_down1,
        sum_gatt,
        sum_wqkv,
        sum_wout,
        sum_gconv,
        sum_point1,
        sum_depth,
        sum_gbn,
        sum_sbn,
        sum_point2,
        sum_gffn2,
        sum_up2,
        sum_down2,
        sum_gfinal,
    ) = shard_grads
    (
        sum_gffn1,
        sum_up1,
        sum_down1,
        sum_gatt,
        sum_wqkv,
        sum_wout,
        sum_table,
        sum_gconv,
        sum_point1,
        sum_depth,
        sum_gbn,
        sum_sbn,
        sum_point2,
        sum_gffn2,
        sum_up2,
        sum_down2,
        sum_gfinal,
    ) = (
        lax.psum(sum_gffn1.astype(jnp.bfloat16), "grp").astype(jnp.float32),
        lax.psum(sum_up1.astype(jnp.bfloat16), "grp").astype(jnp.float32),
        lax.psum(sum_down1.astype(jnp.bfloat16), "grp").astype(jnp.float32),
        lax.psum(sum_gatt.astype(jnp.bfloat16), "grp").astype(jnp.float32),
        lax.psum(sum_wqkv.astype(jnp.bfloat16), "grp").astype(jnp.float32),
        lax.psum(sum_wout.astype(jnp.bfloat16), "grp").astype(jnp.float32),
        lax.psum(grad_table.astype(jnp.bfloat16), "grp").astype(jnp.float32),
        lax.psum(sum_gconv.astype(jnp.bfloat16), "grp").astype(jnp.float32),
        lax.psum(sum_point1.astype(jnp.bfloat16), "grp").astype(jnp.float32),
        lax.psum(sum_depth.astype(jnp.bfloat16), "grp").astype(jnp.float32),
        lax.psum(sum_gbn.astype(jnp.bfloat16), "grp").astype(jnp.float32),
        lax.psum(sum_sbn.astype(jnp.bfloat16), "grp").astype(jnp.float32),
        lax.psum(sum_point2.astype(jnp.bfloat16), "grp").astype(jnp.float32),
        lax.psum(sum_gffn2.astype(jnp.bfloat16), "grp").astype(jnp.float32),
        lax.psum(sum_up2.astype(jnp.bfloat16), "grp").astype(jnp.float32),
        lax.psum(sum_down2.astype(jnp.bfloat16), "grp").astype(jnp.float32),
        lax.psum(sum_gfinal.astype(jnp.bfloat16), "grp").astype(jnp.float32),
    )
    return (
        output,
        input_grad,
        sum_gffn1,
        sum_up1,
        sum_down1,
        sum_gatt,
        sum_wqkv,
        sum_wout,
        sum_table,
        sum_gconv,
        sum_point1,
        sum_depth,
        sum_gbn,
        sum_sbn,
        sum_point2,
        sum_gffn2,
        sum_up2,
        sum_down2,
        sum_gfinal,
    )


def solution(mesh):
    return jax.shard_map(
        per_device,
        mesh=mesh,
        in_specs=(
            P(("grp", "seq"), None),
            P(("grp", "seq"), None),
            P(("grp", "seq"), None),
            P("grp", None),
            P("grp", None),
            P("seq"),
            P("seq", None),
            P("seq", None),
            P("seq"),
            P("seq", None),
            P("seq", None),
            P("seq", None),
            P("seq"),
            P("seq", None),
            P(None, "seq"),
            P("seq"),
            P("seq"),
            P("seq", None),
            P("seq"),
            P("seq", None),
            P("seq", None),
            P("seq"),
        ),
        out_specs=(
            P(("grp", "seq"), None),
            P(("grp", "seq"), None),
            P("seq"),
            P("seq", None),
            P("seq", None),
            P("seq"),
            P("seq", None),
            P("seq", None),
            P("seq", None),
            P("seq"),
            P("seq", None),
            P(None, "seq"),
            P("seq"),
            P("seq"),
            P("seq", None),
            P("seq"),
            P("seq", None),
            P("seq", None),
            P("seq"),
        ),
        check_vma=False,
    )
```

profile of v0, /device:TPU:0, one launch (start us, length us, event | category | flops | bytes accessed | tf_op | source)
XLA Modules:
  0.0 2309.5 jit_solution(7800190122748893116)
XLA Ops:
  32.1 34.8 %all-gather.16.cloned.1.call-done = bf16[1024,4096]{1,0:T(8,128)(2,1)} async-done(((bf16[128,4096]{1,0:T(8,128)(2,1)}), bf16[1024,4096]{1,0:T(8,128)(2,1)}) %all-gather.16.cloned.1.call-update) | async-done | bytes 8388624 | tf_op jit(solution)/shard_map/all_gather | solution.py:183
  74.9 48.2 %all-gather.18.cloned.1.call-done = bf16[4096,1024]{1,0:T(8,128)(2,1)} async-done(((bf16[512,1024]{1,0:T(8,128)(2,1)}), bf16[4096,1024]{1,0:T(8,128)(2,1)}) %all-gather.18.cloned.1.call-update) | async-done | bytes 8388624 | tf_op jit(solution)/shard_map/all_gather | solution.py:184
  130.6 39.9 %all-gather.20.cloned.1.call-done = bf16[1024,3072]{1,0:T(8,128)(2,1)} async-done(((bf16[128,3072]{1,0:T(8,128)(2,1)}), bf16[1024,3072]{1,0:T(8,128)(2,1)}) %all-gather.20.cloned.1.call-update) | async-done | bytes 6291472 | tf_op jit(solution)/shard_map/all_gather | solution.py:186
  185.3 31.1 %all-to-all-done = bf16[256,3,1024]{0,1,2:T(4,128)(2,1)S(1)} async-done(((bf16[256,3,1024]{0,1,2:T(4,128)(2,1)}), bf16[256,3,1024]{0,1,2:T(4,128)(2,1)S(1)}, u32[]{:S(2)}, u32[]{:S(2)}) %all-to-all-start) | async-done | bytes 1572896 | tf_op jit(solution)/shard_map/all_to_all | solution.py:213
  223.5 361.6 %while.33 = (s32[]{:T(128)}, bf16[4,512,1,128]{3,1,2,0:T(8,128)(2,1)}, f32[4,1,512]{2,1,0:T(1,128)S(1)}, s32[4]{0:T(128)S(1)}, s32[2048]{0:T(1024)S(1)}, /*index...) while((s32[]{:T(128)}, ...), condition=%wide.region_10.11_spmd, body=%wide.region_7.10_spmd.sunk | while | flops 548502592 | bytes 55007564 | solution.py:233
  239.9 57.4 %slice_reduce_fusion.4 = f32[1310208]{0:T(1024)} fusion(f32[1,1310720]{1,0:T(1,128)} %bitcast.272), kind=kLoop, calls=%fused_computation.clone.1 | loop fusion | bytes 10481664 | tf_op jit(solution)/shard_map/while/body/eval_jaxpr/slice | solution.py:107
  327.7 57.4 %slice_reduce_fusion.4 = f32[1310208]{0:T(1024)} fusion(f32[1,1310720]{1,0:T(1,128)} %bitcast.272), kind=kLoop, calls=%fused_computation.clone.1 | loop fusion | bytes 10481664 | tf_op jit(solution)/shard_map/while/body/eval_jaxpr/slice | solution.py:107
  415.5 57.4 %slice_reduce_fusion.4 = f32[1310208]{0:T(1024)} fusion(f32[1,1310720]{1,0:T(1,128)} %bitcast.272), kind=kLoop, calls=%fused_computation.clone.1 | loop fusion | bytes 10481664 | tf_op jit(solution)/shard_map/while/body/eval_jaxpr/slice | solution.py:107
  503.2 57.4 %slice_reduce_fusion.4 = f32[1310208]{0:T(1024)} fusion(f32[1,1310720]{1,0:T(1,128)} %bitcast.272), kind=kLoop, calls=%fused_computation.clone.1 | loop fusion | bytes 10481664 | tf_op jit(solution)/shard_map/while/body/eval_jaxpr/slice | solution.py:107
  588.7 12.6 all-gather.2
  659.7 39.3 %psum.147 = f32[1024]{0:T(1024)S(1)} all-reduce(f32[1024]{0:T(1024)S(1)} %get-tuple-element.445), channel_id=1, replica_groups=mesh['grp'=4,'seq'=8] {'grp','seq'}, use_global_device_ids=true, to_apply=%region_14.15 | all-reduce | flops 1024 | bytes 8192 | tf_op jit(solution)/shard_map/psum | solution.py:255
  699.2 40.0 %psum.148 = f32[1024]{0:T(1024)S(1)} all-reduce(f32[1024]{0:T(1024)S(1)} %multiply_reduce_fusion.12), channel_id=1, replica_groups=mesh['grp'=4,'seq'=8] {'grp','seq'}, use_global_device_ids=true, to_apply=%region_16.17 | all-reduce | flops 1024 | bytes 8192 | tf_op jit(solution)/shard_map/psum | solution.py:257
  758.7 10.7 fusion.82
  783.5 40.0 %all-reduce.10 = (f32[1024]{0:T(1024)S(1)}, f32[1024]{0:T(1024)S(1)}) all-reduce(f32[1024]{0:T(1024)S(1)} %get-tuple-element.347, f32[1024]{0:T(1024)S(1)} %get-tuple-element.362), channel_id=1, replica_groups=mesh['grp'=4,'seq'=8] {'grp','seq'}, use_global_device_ids=true, to_apply=%region_28.29 | all-reduce | flops 2048 | bytes 16384 | tf_op jit(solution)/shard_map/psum | solution.py:314
  867.2 756.4 %while.34 = (s32[]{:T(128)}, f32[2048,1,128]{0,2,1:T(8,128)}, f32[2048,1,128]{0,2,1:T(8,128)}, f32[1,32]{1,0:T(1,128)S(1)}, bf16[4,512,1,128]{3,1,2,0:T(8,128)(2...) while((s32[]{:T(128)}, f32[2048,1,128]{0,2,1:T(8,128)}, ...), condition=%wide.region_34.35_spmd.clone, body=%wide.region_31.34_spmd.clone.sunk | while | flops 1359917184 | bytes 168157952 | solution.py:392
  907.8 57.5 %slice_reduce_fusion.5 = f32[1310208]{0:T(1024)} fusion(f32[1,1310720]{1,0:T(1,128)} %bitcast.273), kind=kLoop, calls=%fused_computation.36.clone.1 | loop fusion | bytes 10481664 | tf_op jit(solution)/shard_map/while/body/eval_jaxpr/slice | solution.py:107
  1001.2 56.4 %convert_reduce_fusion.3 = f32[1310720]{0:T(1024)} fusion(bf16[1,1310208]{1,0:T(2,128)(2,1)S(1)} %reshape.691), kind=kLoop, calls=%fused_computation.35.clone.1 | loop fusion | flops 1310720 | bytes 7863296 | tf_op jit(solution)/shard_map/while/body/eval_jaxpr/reshape | solution.py:116
  1089.1 57.5 %slice_reduce_fusion.5 = f32[1310208]{0:T(1024)} fusion(f32[1,1310720]{1,0:T(1,128)} %bitcast.273), kind=kLoop, calls=%fused_computation.36.clone.1 | loop fusion | bytes 10481664 | tf_op jit(solution)/shard_map/while/body/eval_jaxpr/slice | solution.py:107
  1183.3 56.4 %convert_reduce_fusion.3 = f32[1310720]{0:T(1024)} fusion(bf16[1,1310208]{1,0:T(2,128)(2,1)S(1)} %reshape.691), kind=kLoop, calls=%fused_computation.35.clone.1 | loop fusion | flops 1310720 | bytes 7863296 | tf_op jit(solution)/shard_map/while/body/eval_jaxpr/reshape | solution.py:116
  1271.3 57.5 %slice_reduce_fusion.5 = f32[1310208]{0:T(1024)} fusion(f32[1,1310720]{1,0:T(1,128)} %bitcast.273), kind=kLoop, calls=%fused_computation.36.clone.1 | loop fusion | bytes 10481664 | tf_op jit(solution)/shard_map/while/body/eval_jaxpr/slice | solution.py:107
  1365.5 56.4 %convert_reduce_fusion.3 = f32[1310720]{0:T(1024)} fusion(bf16[1,1310208]{1,0:T(2,128)(2,1)S(1)} %reshape.691), kind=kLoop, calls=%fused_computation.35.clone.1 | loop fusion | flops 1310720 | bytes 7863296 | tf_op jit(solution)/shard_map/while/body/eval_jaxpr/reshape | solution.py:116
  1453.4 57.5 %slice_reduce_fusion.5 = f32[1310208]{0:T(1024)} fusion(f32[1,1310720]{1,0:T(1,128)} %bitcast.273), kind=kLoop, calls=%fused_computation.36.clone.1 | loop fusion | bytes 10481664 | tf_op jit(solution)/shard_map/while/body/eval_jaxpr/slice | solution.py:107
  1547.6 56.4 %convert_reduce_fusion.3 = f32[1310720]{0:T(1024)} fusion(bf16[1,1310208]{1,0:T(2,128)(2,1)S(1)} %reshape.691), kind=kLoop, calls=%fused_computation.35.clone.1 | loop fusion | flops 1310720 | bytes 7863296 | tf_op jit(solution)/shard_map/while/body/eval_jaxpr/reshape | solution.py:116
  1637.6 29.1 %all_to_all.65 = bf16[2048,3,128]{2,1,0:T(4,128)(2,1)S(1)} all-to-all(bf16[2048,3,128]{2,1,0:T(4,128)(2,1)S(1)} %copy.89), channel_id=1, replica_groups=mesh['grp'=4,'seq'=8] {'seq'}, dimensions={0} | all-to-all | bytes 3145728 | tf_op jit(solution)/shard_map/all_to_all | solution.py:403
  1734.7 75.0 %reduce-scatter.24.cloned.1.call-done = bf16[128,4096]{1,0:T(8,128)(2,1)} async-done(((bf16[1024,4096]{1,0:T(8,128)(2,1)}), bf16[128,4096]{1,0:T(8,128)(2,1)}) %reduce-scatter.24.cloned.1.call-update) | async-done | bytes 1048592 | tf_op jit(solution)/shard_map/reduce_scatter | solution.py:455
  1809.7 74.8 %reduce-scatter.26.cloned.1.call-done = bf16[512,1024]{1,0:T(8,128)(2,1)} async-done(((bf16[4096,1024]{1,0:T(8,128)(2,1)}), bf16[512,1024]{1,0:T(8,128)(2,1)}) %reduce-scatter.26.cloned.1.call-update) | async-done | bytes 1048592 | tf_op jit(solution)/shard_map/reduce_scatter | solution.py:458
  1884.6 74.8 %reduce-scatter.12.cloned.1.call-done = bf16[128,4096]{1,0:T(8,128)(2,1)} async-done(((bf16[1024,4096]{1,0:T(8,128)(2,1)}), bf16[128,4096]{1,0:T(8,128)(2,1)}) %reduce-scatter.12.cloned.1.call-update) | async-done | bytes 1048592 | tf_op jit(solution)/shard_map/reduce_scatter | solution.py:419
  1959.4 74.8 %reduce-scatter.14.cloned.1.call-done = bf16[512,1024]{1,0:T(8,128)(2,1)} async-done(((bf16[4096,1024]{1,0:T(8,128)(2,1)}), bf16[512,1024]{1,0:T(8,128)(2,1)}) %reduce-scatter.14.cloned.1.call-update) | async-done | bytes 1048592 | tf_op jit(solution)/shard_map/reduce_scatter | solution.py:422
  2035.5 35.8 %reduce-scatter.28.cloned.1.call-done = bf16[128,5]{1,0:T(8,128)(2,1)} async-done(((bf16[1024,5]{1,0:T(8,128)(2,1)}), bf16[128,5]{1,0:T(8,128)(2,1)}) %reduce-scatter.28.cloned.1.call-update) | async-done | bytes 1296
  2079.0 23.8 %all-reduce.11 = (bf16[1024]{0:T(1024)(128)(2,1)S(1)}, bf16[1024]{0:T(1024)(128)(2,1)S(1)}, bf16[1024]{0:T(1024)(128)(2,1)S(1)}, bf16[1024]{0:T(1024)(128)(2,1)S...) all-reduce(bf16[1024]{0:T(1024)(128)(2,1)S(1)} %get-tuple-element.3, ...), channel_id=2, replica_groups=mesh['grp'=4,'seq'=8] {'seq'}, use_global_device_ids=true, to_apply=%region_40.41.clone | all-reduce | flops 7168 | bytes 28672
  2103.4 12.9 all-reduce.12
  2122.3 166.9 %all-reduce.16.cloned.1.call-done = (bf16[128,4096]{1,0:T(8,128)(2,1)}, bf16[512,1024]{1,0:T(8,128)(2,1)}, bf16[128,3072]{1,0:T(8,128)(2,1)}, bf16[128,1024]{1,0...) async-done(((bf16[128,4096]{1,0:T(8,128)(2,1)}, bf16[512,1024]{1,0:T(8,128)(2,1)}, ...) | async-done | bytes 6029328 | tf_op jit(solution)/shard_map/psum | solution.py:503
  (544 shorter events, 698.0 us)
Async XLA Ops:
  7.2 59.7 %all-gather.16.cloned.1.call-start = ((), (), s32[]{:S(2)}) async-start(), calls=%async_computation.13 | async-start | bytes 9437184 | tf_op jit(solution)/shard_map/all_gather | solution.py:183
  8.0 115.2 %all-gather.18.cloned.1.call-start = ((), (), s32[]{:S(2)}) async-start(), calls=%async_computation.14 | async-start | bytes 9437184 | tf_op jit(solution)/shard_map/all_gather | solution.py:184
  8.7 161.7 %all-gather.20.cloned.1.call-start = ((), (), s32[]{:S(2)}) async-start(), calls=%async_computation.15 | async-start | bytes 7077888 | tf_op jit(solution)/shard_map/all_gather | solution.py:186
  9.5 600.9 %all-gather.22.cloned.1.call-start = ((), (), s32[]{:S(2)}) async-start(), calls=%async_computation.16 | async-start | bytes 2359296 | tf_op jit(solution)/shard_map/all_gather | solution.py:187
  10.0 603.2 %all-gather.24.cloned.1.call-start = ((), (), s32[]{:S(2)}) async-start(), calls=%async_computation.17 | async-start | bytes 4718592 | tf_op jit(solution)/shard_map/all_gather | solution.py:189
  10.6 728.5 %all-gather.26.cloned.1.call-start = ((), (), s32[]{:S(2)}) async-start(), calls=%async_computation.18 | async-start | bytes 2359296 | tf_op jit(solution)/shard_map/all_gather | solution.py:193
  11.2 731.1 %all-gather.28.cloned.1.call-start = ((), (), s32[]{:S(2)}) async-start(), calls=%async_computation.19 | async-start | bytes 9437184 | tf_op jit(solution)/shard_map/all_gather | solution.py:195
  31.3 139.1 %copy-start.40 = (f32[8,1,128]{2,1,0:T(1,128)}, f32[8,1,128]{2,1,0:T(1,128)S(1)}, u32[]{:S(2)}) copy-start(f32[8,1,128]{2,1,0:T(1,128)S(1)} %convert_element_type.558) | copy-start | bytes 12292
  130.3 480.0 %copy-start.3 = (f32[256,1024]{1,0:T(8,128)}, f32[256,1024]{1,0:T(8,128)S(1)}, u32[]{:S(2)}) copy-start(f32[256,1024]{1,0:T(8,128)S(1)} %get-tuple-element.470) | copy-start | bytes 3145732
  180.7 35.7 %all-to-all-start = ((bf16[256,3,1024]{0,1,2:T(4,128)(2,1)}), bf16[256,3,1024]{0,1,2:T(4,128)(2,1)S(1)}, u32[]{:S(2)}, u32[]{:S(2)}) async-start(bf16[256,3,1024]{0,1,2:T(4,128)(2,1)} %copy.80), calls=%async_computation | async-start | bytes 4194304 | tf_op jit(solution)/shard_map/all_to_all | solution.py:213
  184.3 565.8 %all-gather.30.cloned.1.call-start = ((), (), s32[]{:S(2)}) async-start(), calls=%async_computation.20 | async-start | bytes 9437184 | tf_op jit(solution)/shard_map/all_gather | solution.py:196
  223.5 365.2 %copy-start.80 = (bf16[128]{0:T(256)(128)(2,1)S(1)}, bf16[128]{0:T(256)(128)(2,1)}, u32[]{:S(2)}) copy-start(bf16[128]{0:T(256)(128)(2,1)} %param.38) | copy-start | bytes 772
  223.5 377.8 %copy-start.72 = (bf16[5,128]{1,0:T(8,128)(2,1)S(1)}, bf16[5,128]{1,0:T(8,128)(2,1)}, u32[]{:S(2)}) copy-start(bf16[5,128]{1,0:T(8,128)(2,1)} %param.40) | copy-start | bytes 3844
  585.1 24.2 %all-to-all-start.1 = ((bf16[8,256,128]{2,1,0:T(8,128)(2,1)}), bf16[8,256,128]{2,1,0:T(8,128)(2,1)S(1)}, u32[]{:S(2)}, u32[]{:S(2)}) async-start(bf16[8,256,128]{2,1,0:T(8,128)(2,1)} %bitcast.26), calls=%async_computation.1 | async-start | bytes 1048576 | tf_op jit(solution)/shard_map/all_to_all | solution.py:235
  588.6 1138.3 %reduce-scatter.22.cloned.1.call-start = ((), (), s32[]{:S(2)}) async-start(), calls=%async_computation.26 | async-start | bytes 2359296 | tf_op jit(solution)/shard_map/reduce_scatter | solution.py:449
  618.5 39.6 %collective-permute-start.1 = (bf16[2,1024]{1,0:T(2,128)(2,1)S(1)}, bf16[2,1024]{1,0:T(2,128)(2,1)S(1)}, u32[]{:S(2)}, u32[]{:S(2)}) collective-permute-start(bf16[2,1024]{1,0:T(2,128)(2,1)S(1)} %get-tuple-element.459), channel_id=1, source_target_pairs={{1,0},{2,1},{3,2},{4,3},{5,4},{6,5},{7,6},{9,8},{10,9},{11,10},{12... | collective-permute-start | bytes 12296 | tf_op jit(solution)/shard_map/ppermute | solution.py:24
  619.8 38.3 %collective-permute-start = (bf16[2,1024]{1,0:T(2,128)(2,1)S(1)}, bf16[2,1024]{1,0:T(2,128)(2,1)S(1)}, u32[]{:S(2)}, u32[]{:S(2)}) collective-permute-start(bf16[2,1024]{1,0:T(2,128)(2,1)S(1)} %get-tuple-element.458), channel_id=1, source_target_pairs={{0,1},{1,2},{2,3},{3,4},{4,5},{5,6},{6,7},{8,9},{9,10},{10,11},{11... | collective-permute-start | bytes 12296 | tf_op jit(solution)/shard_map/ppermute | solution.py:21
  649.2 124.7 %copy-start.36 = (f32[8,1,128]{2,1,0:T(1,128)}, f32[8,1,128]{2,1,0:T(1,128)S(1)}, u32[]{:S(2)}) copy-start(f32[8,1,128]{2,1,0:T(1,128)S(1)} %convert_element_type.562) | copy-start | bytes 12292
  658.1 115.9 %copy-start.42 = (f32[8,1,128]{2,1,0:T(1,128)}, f32[8,1,128]{2,1,0:T(1,128)S(1)}, u32[]{:S(2)}) copy-start(f32[8,1,128]{2,1,0:T(1,128)S(1)} %convert_element_type.563) | copy-start | bytes 12292
  823.6 903.4 %reduce-scatter.18.cloned.1.call-start = ((), (), s32[]{:S(2)}) async-start(), calls=%async_computation.24 | async-start | bytes 2359296 | tf_op jit(solution)/shard_map/reduce_scatter | solution.py:431
  829.1 2.9 collective-permute-start.3
  830.7 5.6 collective-permute-start.2
  848.3 18.0 all-to-all-start.2
  854.0 873.0 %reduce-scatter.20.cloned.1.call-start = ((), (), s32[]{:S(2)}) async-start(), calls=%async_computation.25 | async-start | bytes 4718592 | tf_op jit(solution)/shard_map/reduce_scatter | solution.py:437
  858.6 876.1 %reduce-scatter.16.cloned.1.call-start = ((), (), s32[]{:S(2)}) async-start(), calls=%async_computation.23 | async-start | bytes 7077888 | tf_op jit(solution)/shard_map/reduce_scatter | solution.py:428
  1674.7 135.0 %reduce-scatter.24.cloned.1.call-start = ((), (), s32[]{:S(2)}) async-start(), calls=%async_computation.27 | async-start | bytes 9437184 | tf_op jit(solution)/shard_map/reduce_scatter | solution.py:455
  1684.2 200.3 %reduce-scatter.26.cloned.1.call-start = ((), (), s32[]{:S(2)}) async-start(), calls=%async_computation.28 | async-start | bytes 9437184 | tf_op jit(solution)/shard_map/reduce_scatter | solution.py:458
  1694.5 264.9 %reduce-scatter.12.cloned.1.call-start = ((), (), s32[]{:S(2)}) async-start(), calls=%async_computation.21 | async-start | bytes 9437184 | tf_op jit(solution)/shard_map/reduce_scatter | solution.py:419
  1716.8 317.4 %reduce-scatter.14.cloned.1.call-start = ((), (), s32[]{:S(2)}) async-start(), calls=%async_computation.22 | async-start | bytes 9437184 | tf_op jit(solution)/shard_map/reduce_scatter | solution.py:422
  1725.2 309.0 %copy-start.88 = (u32[32]{0:T(128)S(1)}, u32[32]{0:T(128)}, u32[]{:S(2)}) copy-start(u32[32]{0:T(128)} %constant.288) | copy-start | bytes 388
  1725.2 346.1 %reduce-scatter.28.cloned.1.call-start = ((), (), s32[]{:S(2)}) async-start(), calls=%async_computation.29 | async-start | bytes 294912
  1726.9 562.3 %all-reduce.16.cloned.1.call-start = ((), (), s32[]{:S(2)}) async-start(), calls=%async_computation.30 | async-start | bytes 12058624 | tf_op jit(solution)/shard_map/psum | solution.py:503
  (94 other events, 1084.0 us)
Sparse Core Ops, SparseCore 0:
  9.9 56.9 all-gather.15
  68.9 54.2 all-gather.17
  125.0 45.3 all-gather.19
  172.2 38.8 all-gather.21
  212.9 36.6 all-gather.23
  251.3 27.7 all-gather.25
  281.0 54.2 all-gather.27
  337.2 54.2 all-gather.29
  823.7 43.4 reduce-scatter.21
  870.9 39.6 reduce-scatter.17
  914.0 51.1 reduce-scatter.19
  1674.8 59.8 reduce-scatter.15
  1738.2 71.4 reduce-scatter.23
  1813.0 71.4 reduce-scatter.25
  1887.9 71.4 reduce-scatter.11
  1962.7 71.4 reduce-scatter.13
  2037.7 33.6 reduce-scatter.27
  2074.2 215.0 all-reduce.15
where the time goes:
time: 2320 us; the launch traced here: 2310 us
  local copies, waits for them, and re-layouts  772 us (33%)
  waiting for transfers between devices  681 us (29%)
  other arithmetic  279 us (12%)
  blocking collectives  260 us (11%)
  matrix products  235 us (10%)
  loops' own time  44.6 us (2%)
    slice x8, local copies, waits for them, and re-layouts, relative_bias(): bias_tiles[:, :block_len * span_len]  460 us
    reshape x4, other arithmetic, diagonal_sums(): flat_grads.reshape(heads_here, block_len, span_len + 1)  226 us
    psum x1, waiting for transfers between devices, per_device(): lax.psum(sum_up1.astype(jnp.bfloat16), 'grp').astype(jnp.float32)  167 us
    while x44, local copies, waits for them, and re-layouts  140 us
    reduce_scatter x1, waiting for transfers between devices, per_device(): lax.psum_scatter(grad_up2.astype(jnp.bfloat16), 'seq', scatter_dimension=...  75 us
    reduce_scatter x1, waiting for transfers between devices, per_device(): lax.psum_scatter(grad_down1.astype(jnp.bfloat16), 'seq', scatter_dimensio...  74.8 us
    reduce_scatter x1, waiting for transfers between devices, per_device(): lax.psum_scatter(grad_down2.astype(jnp.bfloat16), 'seq', scatter_dimensio...  74.8 us
    reduce_scatter x1, waiting for transfers between devices, per_device(): lax.psum_scatter(grad_up1.astype(jnp.bfloat16), 'seq', scatter_dimension=...  74.8 us
  transfers between devices with their start and end apart: 25, of which 13 were waited for; matrix products, arithmetic and copies ran while one was open for 53% of the time, Pallas kernels for 0%

commit v1 on v0

v1 whole, which is shorter than its diff:
```python
import functools

import jax
import jax.numpy as jnp
from jax import lax
from jax.experimental import pallas as pl
from jax.experimental.pallas import tpu as pltpu
from jax.sharding import PartitionSpec as P

KERNEL = 5
SPAN_LEN = 10
HEAD_DIM = 128
BLK = 256
REACH = 4
TILES = 2 * REACH + 1
LOG2E = 1.4426950408889634

epsilon = 1e-05
limits = (8, 16, 32, 64, 128, 256, 512, 1024)
highest = lax.Precision.HIGHEST
bf16 = jnp.bfloat16
f32 = jnp.float32


def bucket_of(distance):
    magnitude = jnp.abs(distance)
    result = jnp.minimum(magnitude, 7)
    for bound_at in limits:
        result = result + (magnitude >= bound_at).astype(jnp.int32)
    return result + 16 * (distance > 0).astype(jnp.int32)


def normalize(tensor, gain_vec):
    centred = tensor - jnp.mean(tensor, axis=-1, keepdims=True)
    factor = lax.rsqrt(jnp.mean(centred * centred, axis=-1, keepdims=True) + epsilon)
    normed = centred * factor
    return (normed * gain_vec, normed, factor)


def normalize_back(grad_out, normed, factor, gain_vec):
    grad_gain = jnp.sum(grad_out * normed, axis=0)
    scaled = grad_out * gain_vec
    grad_in = factor * (
        scaled
        - jnp.mean(scaled, axis=-1, keepdims=True)
        - normed * jnp.mean(scaled * normed, axis=-1, keepdims=True)
    )
    return (grad_in, grad_gain)


def contract(left, right, left_dim, right_dim):
    return lax.dot_general(
        left, right, (((left_dim,), (right_dim,)), ((), ())), preferred_element_type=f32
    )


def matmul(left, right):
    return contract(left, right, 1, 0)


def left_product(left, right):
    return contract(left, right, 0, 0)


def right_product(left, right):
    return contract(left, right, 1, 1)


def swish_slope(pre_act):
    sig_val = jax.nn.sigmoid(pre_act)
    return sig_val * (1.0 + pre_act * (1.0 - sig_val))


def masked_scores(q, k, tile, key_at, begin, end, scale):
    scores = right_product(k, q) * scale + tile
    return jnp.where((key_at >= begin) & (key_at < end), scores, -1e30)


def fill_tiles(line_ref, tiles_ref):
    for t in range(TILES):
        row = jnp.broadcast_to(line_ref[t : t + 1, :], (BLK, 2 * BLK))
        tiles_ref[t] = pltpu.roll(row, 0, 1, stride=1, stride_axis=0)[:, :BLK]


def attend_kernel(
    scale, low_ref, high_ref, q_ref, k_ref, v_ref, begin_ref, end_ref, line_ref,
    out_ref, lse_ref, tiles_ref,
):
    i = pl.program_id(0)

    @pl.when(i == 0)
    def _():
        fill_tiles(line_ref, tiles_ref)

    q = q_ref[...]
    begin = begin_ref[...]
    end = end_ref[...]
    row_at = lax.broadcasted_iota(jnp.int32, (BLK, BLK), 0)

    def step(j, carry):
        peak, total, acc = carry
        at = pl.multiple_of(j * BLK, BLK)
        keys = k_ref[pl.ds(at, BLK), :]
        scores = masked_scores(
            q, keys, tiles_ref[j - i + REACH], row_at + at, begin, end, scale
        )
        peak_new = jnp.maximum(peak, jnp.max(scores, axis=0, keepdims=True))
        probs = jnp.exp2(scores - peak_new)
        shrink = jnp.exp2(peak - peak_new)
        total = total * shrink + jnp.sum(probs, axis=0, keepdims=True)
        acc = acc * shrink + left_product(v_ref[pl.ds(at, BLK), :], probs.astype(bf16))
        return peak_new, total, acc

    first = (
        jnp.full((1, BLK), -1e30, f32),
        jnp.zeros((1, BLK), f32),
        jnp.zeros((HEAD_DIM, BLK), f32),
    )
    peak, total, acc = lax.fori_loop(low_ref[i], high_ref[i], step, first)
    out_ref[...] = (acc / total).T
    lse_ref[...] = peak + jnp.log2(total)


def attend_back_kernel(
    scale, plain, low_ref, high_ref, q_ref, k_ref, v_ref, go_ref, out_ref, lse_ref,
    begin_ref, end_ref, line_ref, grad_ref, diag_ref, tiles_ref, sums_ref, gk_ref, gv_ref,
):
    i = pl.program_id(0)

    @pl.when(i == 0)
    def _():
        fill_tiles(line_ref, tiles_ref)
        sums_ref[...] = jnp.zeros_like(sums_ref)
        gk_ref[...] = jnp.zeros_like(gk_ref)
        gv_ref[...] = jnp.zeros_like(gv_ref)

    q = q_ref[...]
    go = go_ref[...]
    begin = begin_ref[...]
    end = end_ref[...]
    lse = lse_ref[...]
    delta = lax.dot_general(
        jnp.ones((8, HEAD_DIM), f32), go.astype(f32) * out_ref[...],
        (((1,), (1,)), ((), ())), precision=highest, preferred_element_type=f32,
    )[0:1, :]
    row_at = lax.broadcasted_iota(jnp.int32, (BLK, BLK), 0)

    def step(j, gq):
        at = pl.multiple_of(j * BLK, BLK)
        rows = pl.ds(at, BLK)
        keys = k_ref[rows, :]
        scores = masked_scores(
            q, keys, tiles_ref[j - i + REACH], row_at + at, begin, end, scale
        )
        probs = jnp.exp2(scores - lse)
        gp = right_product(v_ref[rows, :], go)
        gs = (probs * (gp - delta)).astype(bf16)
        gv_ref[rows, :] += matmul(probs.astype(bf16), go)
        gk_ref[rows, :] += matmul(gs, q)
        sums_ref[j - i + REACH] += gs.astype(f32)
        return gq + left_product(gs, keys)

    gq = lax.fori_loop(low_ref[i], high_ref[i], step, jnp.zeros((BLK, HEAD_DIM), f32))
    grad_ref[pl.ds(pl.multiple_of(i * BLK, BLK), BLK), 0:HEAD_DIM] = (gq * plain).astype(bf16)

    @pl.when(i == pl.num_programs(0) - 1)
    def _():
        grad_ref[:, HEAD_DIM : 2 * HEAD_DIM] = (gk_ref[...] * plain).astype(bf16)
        grad_ref[:, 2 * HEAD_DIM :] = gv_ref[...].astype(bf16)
        back_at = lax.broadcasted_iota(jnp.int32, (BLK, 2 * BLK), 0)
        for t in range(TILES):
            wide = jnp.concatenate([sums_ref[t], jnp.zeros((BLK, BLK), f32)], axis=1)
            bit = 1
            while bit < BLK:
                moved = pltpu.roll(wide, 2 * BLK - bit, 1)
                wide = jnp.where((back_at // bit) % 2 == 1, moved, wide)
                bit *= 2
            diag_ref[t : t + 1, :] = jnp.sum(wide, axis=0, keepdims=True)
        diag_ref[TILES:, :] = jnp.zeros((16 - TILES, 2 * BLK), f32)


def column(at):
    return pl.BlockSpec((BLK, HEAD_DIM), lambda i, low, high: (i, at))


def whole(at, rows):
    return pl.BlockSpec((rows, HEAD_DIM), lambda i, low, high: (0, at))


def line_row():
    return pl.BlockSpec((1, BLK), lambda i, low, high: (0, i))


def fixed(shape):
    return pl.BlockSpec(shape, lambda i, low, high: (0, 0))


def attend(qkv, low, high, begin, end, line):
    rows = qkv.shape[0]
    scale = HEAD_DIM ** (-0.5) * LOG2E
    return pl.pallas_call(
        functools.partial(attend_kernel, scale),
        out_shape=(
            jax.ShapeDtypeStruct((rows, HEAD_DIM), f32),
            jax.ShapeDtypeStruct((1, rows), f32),
        ),
        grid_spec=pltpu.PrefetchScalarGridSpec(
            num_scalar_prefetch=2,
            grid=(rows // BLK,),
            in_specs=[
                column(0), whole(1, rows), whole(2, rows),
                line_row(), line_row(), fixed((16, 2 * BLK)),
            ],
            out_specs=(column(0), line_row()),
            scratch_shapes=[pltpu.VMEM((TILES, BLK, BLK), f32)],
        ),
        name="attend",
    )(low, high, qkv, qkv, qkv, begin, end, line)


def attend_back(qkv, grad_out, out, lse, low, high, begin, end, line):
    rows = qkv.shape[0]
    plain = HEAD_DIM ** (-0.5)
    return pl.pallas_call(
        functools.partial(attend_back_kernel, plain * LOG2E, plain),
        out_shape=(
            jax.ShapeDtypeStruct((rows, 3 * HEAD_DIM), bf16),
            jax.ShapeDtypeStruct((16, 2 * BLK), f32),
        ),
        grid_spec=pltpu.PrefetchScalarGridSpec(
            num_scalar_prefetch=2,
            grid=(rows // BLK,),
            in_specs=[
                column(0), whole(1, rows), whole(2, rows), column(0), column(0),
                line_row(), line_row(), line_row(), fixed((16, 2 * BLK)),
            ],
            out_specs=(fixed((rows, 3 * HEAD_DIM)), fixed((16, 2 * BLK))),
            scratch_shapes=[
                pltpu.VMEM((TILES, BLK, BLK), f32),
                pltpu.VMEM((TILES, BLK, BLK), f32),
                pltpu.VMEM((rows, HEAD_DIM), f32),
                pltpu.VMEM((rows, HEAD_DIM), f32),
            ],
        ),
        name="attend_back",
    )(low, high, qkv, qkv, qkv, grad_out, out, lse, begin, end, line)


def gather_rows(block):
    return lax.all_gather(block, "seq", axis=0, tiled=True)


def scatter_rows(partial):
    return lax.psum_scatter(
        partial.astype(bf16), "seq", scatter_dimension=0, tiled=True
    ).astype(f32)


def own_columns(weight, parts):
    count = lax.axis_size("seq")
    rows, width = weight.shape
    split = weight.reshape(rows, parts, count, width // (parts * count))
    moved = lax.all_to_all(split, "seq", split_axis=2, concat_axis=0, tiled=True)
    return moved.reshape(rows * count, width // count)


def own_rows(grad, parts):
    count = lax.axis_size("seq")
    rows, width = grad.shape
    split = grad.astype(bf16).reshape(rows, parts, 1, width // parts)
    moved = lax.all_to_all(split, "seq", split_axis=0, concat_axis=2, tiled=True)
    return moved.reshape(rows // count, width * count)


def grp_sum(value):
    return lax.psum(value.astype(bf16), "grp").astype(f32)


def per_device(
    inputs, noise, cotangent, lengths, span_starts,
    ffn1_gain, ffn1_up, ffn1_down, att_gain, qkv_weight, out_weight, rel_bias,
    conv_gain, point1_weight, depth_weight, bn_gain, bn_shift, point2_weight,
    ffn2_gain, ffn2_up, ffn2_down, final_gain,
):
    frame_count = inputs.shape[0]
    count = lax.axis_size("seq")
    groups = lax.axis_size("grp")
    group_len = frame_count * count
    total_len = group_len * groups
    offset = lax.axis_index("seq") * frame_count
    gains = lax.all_gather(
        jnp.stack([ffn1_gain, att_gain, conv_gain, ffn2_gain, final_gain]),
        "seq", axis=1, tiled=True,
    ).astype(f32)
    up_one = own_columns(ffn1_up, 1)
    w_qkv = own_columns(qkv_weight, 3)
    w_point1 = own_columns(point1_weight, 2)
    up_two = own_columns(ffn2_up, 1)

    ends = jnp.cumsum(lengths[0])
    starts = ends - lengths[0]
    places = jnp.arange(group_len, dtype=jnp.int32)
    inside = (places[:, None] >= starts[None, :]) & (places[:, None] < ends[None, :])
    begin = jnp.sum(jnp.where(inside, starts[None, :], 0), axis=1)
    end = jnp.sum(jnp.where(inside, ends[None, :], 0), axis=1)
    low = begin[::BLK] // BLK
    high = (end[BLK - 1 :: BLK] + BLK - 1) // BLK
    begin_row = begin[None, :]
    end_row = end[None, :]
    delta_at = (jnp.arange(16, dtype=jnp.int32) - REACH)[:, None] * BLK
    lane_at = jnp.arange(2 * BLK, dtype=jnp.int32)[None, :]
    lane_at = jnp.where(lane_at < BLK, lane_at, lane_at - 2 * BLK)
    bucket = bucket_of(delta_at - lane_at).reshape(-1)
    onehot = (bucket[None, :] == jnp.arange(rel_bias.shape[1], dtype=jnp.int32)[:, None]).astype(f32)
    line = jnp.dot(rel_bias.astype(f32) * LOG2E, onehot, precision=highest).reshape(16, 2 * BLK)

    local_at = offset + jnp.arange(frame_count, dtype=jnp.int32)
    begins = span_starts[0]
    covered = jnp.any(
        (local_at[:, None] >= begins[None, :]) & (local_at[:, None] < begins[None, :] + SPAN_LEN),
        axis=1,
    )[:, None]

    def ffn_forward(hidden, gain_vec, up_proj, down_proj):
        normal_out, normed, factor = normalize(hidden, gain_vec)
        full = gather_rows(normal_out.astype(bf16))
        pre_act = matmul(full, up_proj)
        inner = jax.nn.silu(pre_act).astype(bf16)
        result = hidden + 0.5 * scatter_rows(matmul(inner, down_proj))
        return result, (full, pre_act, inner, normed, factor)

    def ffn_backward(grad_h, saved, gain_vec, up_proj, down_proj):
        full, pre_act, inner, normed, factor = saved
        branch = gather_rows((0.5 * grad_h).astype(bf16))
        grad_down = left_product(inner, branch)
        grad_pre = (right_product(branch, down_proj) * swish_slope(pre_act)).astype(bf16)
        grad_up = left_product(full, grad_pre)
        grad_in, grad_gain = normalize_back(
            scatter_rows(right_product(grad_pre, up_proj)), normed, factor, gain_vec
        )
        return grad_h + grad_in, grad_gain, grp_sum(own_rows(grad_up, 1)), grp_sum(grad_down)

    hidden_zero = jnp.where(covered, noise.astype(f32), inputs.astype(f32))
    hidden_one, saved_one = ffn_forward(hidden_zero, gains[0], up_one, ffn1_down)

    att_out, att_normed, att_factor = normalize(hidden_one, gains[1])
    att_full = gather_rows(att_out.astype(bf16))
    qkv = matmul(att_full, w_qkv).astype(bf16)
    att_exact, lse = attend(qkv, low, high, begin_row, end_row, line)
    attended = att_exact.astype(bf16)
    hidden_two = hidden_one + scatter_rows(matmul(attended, out_weight))

    conv_out, conv_normed, conv_factor = normalize(hidden_two, gains[2])
    conv_full = gather_rows(conv_out.astype(bf16))
    gated = matmul(conv_full, w_point1)
    width = gated.shape[1] // 2
    linear_part = gated[:, :width]
    sig_gate = jax.nn.sigmoid(gated[:, width:])
    glu = (linear_part * sig_gate).astype(bf16).astype(f32)
    taps = depth_weight.astype(f32)

    def shifted(value, shift):
        at = places + shift
        same = ((at >= begin) & (at < end))[:, None]
        padded = jnp.pad(value, ((2, 2), (0, 0)))
        return jnp.where(same, padded[2 + shift : 2 + shift + group_len], 0.0)

    conv_sum = sum(taps[k] * shifted(glu, k - 2) for k in range(KERNEL))
    mean_c = lax.psum(jnp.sum(conv_sum, axis=0), "grp") / total_len
    centred = conv_sum - mean_c
    var_c = lax.psum(jnp.sum(centred * centred, axis=0), "grp") / total_len
    inv_std = lax.rsqrt(var_c + epsilon)
    normed_bn = centred * inv_std
    gain_bn = bn_gain.astype(f32)
    bn_value = normed_bn * gain_bn + bn_shift.astype(f32)
    swished = jax.nn.silu(bn_value).astype(bf16)
    hidden_three = hidden_two + scatter_rows(matmul(swished, point2_weight))

    hidden_four, saved_two = ffn_forward(hidden_three, gains[3], up_two, ffn2_down)
    final_out, final_normed, final_factor = normalize(hidden_four, gains[4])
    output = final_out.astype(bf16)

    grad_four, grad_gfinal = normalize_back(
        cotangent.astype(f32), final_normed, final_factor, gains[4]
    )
    grad_three, grad_gffn2, grad_up2, grad_down2 = ffn_backward(
        grad_four, saved_two, gains[3], up_two, ffn2_down
    )

    branch = gather_rows(grad_three.astype(bf16))
    grad_point2 = grp_sum(left_product(swished, branch))
    grad_bn = right_product(branch, point2_weight) * swish_slope(bn_value)
    grad_gain_bn, grad_shift_bn = lax.psum(
        (jnp.sum(grad_bn * normed_bn, axis=0), jnp.sum(grad_bn, axis=0)), "grp"
    )
    grad_conv = (
        inv_std
        * gain_bn
        * (grad_bn - grad_shift_bn / total_len - normed_bn * (grad_gain_bn / total_len))
    ).astype(bf16).astype(f32)
    grad_depth = jnp.stack(
        [jnp.sum(grad_conv * shifted(glu, k - 2), axis=0) for k in range(KERNEL)]
    )
    grad_glu = sum(taps[k] * shifted(grad_conv, 2 - k) for k in range(KERNEL))
    grad_gated = jnp.concatenate(
        [grad_glu * sig_gate, grad_glu * linear_part * sig_gate * (1.0 - sig_gate)], axis=1
    ).astype(bf16)
    grad_point1 = grp_sum(own_rows(left_product(conv_full, grad_gated), 2))
    grad_in3, grad_gconv = normalize_back(
        scatter_rows(right_product(grad_gated, w_point1)), conv_normed, conv_factor, gains[2]
    )
    grad_two = grad_three + grad_in3

    grad_att = gather_rows(grad_two.astype(bf16))
    grad_wout = grp_sum(left_product(attended, grad_att))
    grad_attended = right_product(grad_att, out_weight).astype(bf16)
    grad_qkv, diag = attend_back(
        qkv, grad_attended, att_exact, lse, low, high, begin_row, end_row, line
    )
    grad_table = jnp.dot(diag.reshape(1, -1), onehot.T, precision=highest)
    grad_wqkv = grp_sum(own_rows(left_product(att_full, grad_qkv), 3))
    grad_in2, grad_gatt = normalize_back(
        scatter_rows(right_product(grad_qkv, w_qkv)), att_normed, att_factor, gains[1]
    )
    grad_one = grad_two + grad_in2
    grad_zero, grad_gffn1, grad_up1, grad_down1 = ffn_backward(
        grad_one, saved_one, gains[0], up_one, ffn1_down
    )
    input_grad = jnp.where(covered, 0.0, grad_zero).astype(bf16)
    gain_grads = lax.psum_scatter(
        jnp.stack([grad_gffn1, grad_gatt, grad_gconv, grad_gffn2, grad_gfinal]),
        "seq", scatter_dimension=1, tiled=True,
    )
    gain_grads, grad_depth, grad_table = lax.psum((gain_grads, grad_depth, grad_table), "grp")
    return (
        output, input_grad, gain_grads[0], grad_up1, grad_down1, gain_grads[1], grad_wqkv,
        grad_wout, grad_table, gain_grads[2], grad_point1, grad_depth, grad_gain_bn,
        grad_shift_bn, grad_point2, gain_grads[3], grad_up2, grad_down2, gain_grads[4],
    )


def solution(mesh):
    rows, seq, flat = P(("grp", "seq"), None), P("seq", None), P("seq")
    table, taps, per_group = P("seq", None), P(None, "seq"), P("grp", None)
    return jax.shard_map(
        per_device,
        mesh=mesh,
        in_specs=(
            rows, rows, rows, per_group, per_group, flat, seq, seq, flat, seq, seq, table,
            flat, seq, taps, flat, flat, seq, flat, seq, seq, flat,
        ),
        out_specs=(
            rows, rows, flat, seq, seq, flat, seq, seq, table, flat, seq, taps, flat, flat,
            seq, flat, seq, seq, flat,
        ),
        check_vma=False,
    )
```

time: 2320 us -> 1290 us (0.56)
  local copies, waits for them, and re-layouts: 772 us -> 56.1 us
  other arithmetic: 279 us -> 65.9 us
  waiting for transfers between devices: 681 us -> 858 us
  blocking collectives: 260 us -> 104 us
  matrix products: 235 us -> 118 us
  loops' own time: 44.6 us -> 0 us
  Pallas kernels: 0 us -> 44.1 us
    slice x12 -> x3, local copies, waits for them, and re-layouts: 462 us -> 0.19 us  [the longest x1 0.09 us: per_device(): high = (end[BLK - 1::BLK] + BLK - 1) // BLK]
    reshape x4 -> x2, other arithmetic: 226 us -> 2.99 us  [own_rows(): split = grad.astype(bf16).reshape(rows, parts, 1, width // parts)]
    while x46 -> x0, local copies, waits for them, and re-layouts: 143 us -> none
    dot_general x64 -> x26, matrix products: 235 us -> 118 us  [the longest x24 117 us: contract(): lax.dot_general(left, right, (((left_dim,), (right_dim,)), ((), ())), pre...]
    reshape x17 -> x7, local copies, waits for them, and re-layouts: 115 us -> 7.05 us  [the longest x3 3.05 us: own_rows(): split = grad.astype(bf16).reshape(rows, parts, 1, width // parts)]
    all_gather x8, waiting for transfers between devices: 123 us -> 222 us  [gather_rows(): return lax.all_gather(block, 'seq', axis=0, tiled=True)]
    psum x4, blocking collectives: 132 us -> 44.3 us  [the longest x1 12.6 us: per_device(): lax.psum((gain_grads, grad_depth, grad_table), 'grp')]
    reduce_scatter x8 -> x9, waiting for transfers between devices: 307 us -> 372 us  [the longest x8 360 us: scatter_rows(): lax.psum_scatter(partial.astype(bf16), 'seq', scatter_dimension=0, tiled=...]
  transfers between devices with their start and end apart: 25 -> 24, of which waited for: 13 -> 23; matrix products, arithmetic and copies ran while one was open for 53% -> 7% of each run, Pallas kernels for 0% -> 0%
where the time goes in v1:
time: 1290 us
  waiting for transfers between devices  858 us (67%)
  matrix products  118 us (9%)
  blocking collectives  104 us (8%)
  other arithmetic  65.9 us (5%)
  local copies, waits for them, and re-layouts  56.1 us (4%)
  Pallas kernels  44.1 us (3%)
  starting transfers between devices  23.6 us (2%)
  between operations  15.6 us (1%)
    reduce_scatter x8, waiting for transfers between devices, scatter_rows(): lax.psum_scatter(partial.astype(bf16), 'seq', scatter_dimension=0, tiled=...  360 us
    all_gather x8, waiting for transfers between devices, gather_rows(): return lax.all_gather(block, 'seq', axis=0, tiled=True)  222 us
    psum x1, waiting for transfers between devices, grp_sum(): return lax.psum(value.astype(bf16), 'grp').astype(f32)  206 us
    dot_general x24, matrix products, contract(): lax.dot_general(left, right, (((left_dim,), (right_dim,)), ((), ())), pre...  117 us
    all_to_all x2, blocking collectives, own_columns(): lax.all_to_all(split, 'seq', split_axis=2, concat_axis=0, tiled=True)  49.1 us
    unnamed x158, local copies, waits for them, and re-layouts  36.7 us
    all_to_all x4, waiting for transfers between devices, own_rows(): lax.all_to_all(split, 'seq', split_axis=0, concat_axis=2, tiled=True)  29.4 us
    all_to_all x2, waiting for transfers between devices, own_columns(): lax.all_to_all(split, 'seq', split_axis=2, concat_axis=0, tiled=True)  27.7 us
  transfers between devices with their start and end apart: 24, of which 23 were waited for; matrix products, arithmetic and copies ran while one was open for 7% of the time, Pallas kernels for 0%

profile of v1, /device:TPU:0, one launch (start us, length us, event | category | flops | bytes accessed | tf_op | source)
XLA Modules:
  0.0 1285.2 jit_solution(14568142788409241912)
XLA Ops:
  12.6 10.4 all_gather.27
  26.7 23.5 %all_to_all.120 = bf16[128,1,8,512]{0,3,1,2:T(8,128)(2,1)S(1)} all-to-all(bf16[128,1,8,512]{0,3,1,2:T(8,128)(2,1)S(1)} %bitcast.180), channel_id=1, replica_groups=mesh['grp'=4,'seq'=8] {'seq'}, dimensions={2} | all-to-all | bytes 2097152 | tf_op jit(solution)/shard_map/all_to_all | solution.py:263
  50.8 19.3 %all-gather.9.cloned.1.call-done = bf16[2048,1024]{1,0:T(8,128)(2,1)} async-done(((bf16[256,1024]{1,0:T(8,128)(2,1)}), bf16[2048,1024]{1,0:T(8,128)(2,1)}) %all-gather.9.cloned.1.call-update) | async-done | bytes 4194320 | tf_op jit(solution)/shard_map/all_gather | solution.py:250
  81.2 51.2 %reduce-scatter.10.cloned.1.call-done = bf16[256,1024]{1,0:T(8,128)(2,1)} async-done(((bf16[2048,1024]{1,0:T(8,128)(2,1)}), bf16[256,1024]{1,0:T(8,128)(2,1)}) %reduce-scatter.10.cloned.1.call-update) | async-done | bytes 524304 | tf_op jit(solution)/shard_map/reduce_scatter | solution.py:254
  143.6 15.6 %all-to-all-done.1 = bf16[128,3,8,128]{0,3,1,2:T(8,128)(2,1)S(1)} async-done(((bf16[128,3,8,128]{0,3,1,2:T(8,128)(2,1)}), bf16[128,3,8,128]{0,3,1,2:T(8,128)(2,1)S(1)}, u32[]{:S(2)}, u32[]{:S(2)}) %all-to-all-start.1) | async-done | bytes 786464 | tf_op jit(solution)/shard_map/all_to_all | solution.py:263
  160.7 18.2 %all-gather.11.cloned.1.call-done = bf16[2048,1024]{1,0:T(8,128)(2,1)} async-done(((bf16[256,1024]{1,0:T(8,128)(2,1)}), bf16[2048,1024]{1,0:T(8,128)(2,1)}) %all-gather.11.cloned.1.call-update) | async-done | bytes 4194320 | tf_op jit(solution)/shard_map/all_gather | solution.py:250
  184.8 16.9 %attend.1 = (f32[2048,128]{1,0:T(8,128)}, f32[1,2048]{1,0:T(1,128)}) custom-call(s32[8]{0:T(128)} %get-tuple-element.146.low_ref, s32[8]{0:T(128)} %get-tuple-element.145.high_ref, bf16[2048,384]{1,0:T(8,128)(2,1)} %convolution_convert_fusion.8.q_ref.k_ref.v_ref, bf16[2048,384]{1,0:T(8,128)(2,1)} %convolution_convert_fusion.8.q_ref.k_ref.v_ref, ...), custom_call_target="tpu_custom_call" | custom-call | tf_op jit(solution)/shard_map/attend/pallas_call | solution.py:201
  206.3 53.8 %reduce-scatter.12.cloned.1.call-done = bf16[256,1024]{1,0:T(8,128)(2,1)} async-done(((bf16[2048,1024]{1,0:T(8,128)(2,1)}), bf16[256,1024]{1,0:T(8,128)(2,1)}) %reduce-scatter.12.cloned.1.call-update) | async-done | bytes 524304 | tf_op jit(solution)/shard_map/reduce_scatter | solution.py:254
  269.0 12.1 all-to-all-done.2
  281.4 21.3 %all-gather.13.cloned.1.call-done = bf16[2048,1024]{1,0:T(8,128)(2,1)} async-done(((bf16[256,1024]{1,0:T(8,128)(2,1)}), bf16[2048,1024]{1,0:T(8,128)(2,1)}) %all-gather.13.cloned.1.call-update) | async-done | bytes 4194320 | tf_op jit(solution)/shard_map/all_gather | solution.py:250
  310.8 11.7 psum.105
  322.8 8.4 psum.106
  336.0 49.9 %reduce-scatter.14.cloned.1.call-done = bf16[256,1024]{1,0:T(8,128)(2,1)} async-done(((bf16[2048,1024]{1,0:T(8,128)(2,1)}), bf16[256,1024]{1,0:T(8,128)(2,1)}) %reduce-scatter.14.cloned.1.call-update) | async-done | bytes 524304 | tf_op jit(solution)/shard_map/reduce_scatter | solution.py:254
  391.0 25.6 %all_to_all.121 = bf16[128,1,8,512]{0,3,1,2:T(8,128)(2,1)} all-to-all(bf16[128,1,8,512]{0,3,1,2:T(8,128)(2,1)} %bitcast.181), channel_id=1, replica_groups=mesh['grp'=4,'seq'=8] {'seq'}, dimensions={2} | all-to-all | bytes 2097152 | tf_op jit(solution)/shard_map/all_to_all | solution.py:263
  418.9 17.2 %all-gather.15.cloned.1.call-done = bf16[2048,1024]{1,0:T(8,128)(2,1)} async-done(((bf16[256,1024]{1,0:T(8,128)(2,1)}), bf16[2048,1024]{1,0:T(8,128)(2,1)}) %all-gather.15.cloned.1.call-update) | async-done | bytes 4194320 | tf_op jit(solution)/shard_map/all_gather | solution.py:250
  447.5 51.3 %reduce-scatter.16.cloned.1.call-done = bf16[256,1024]{1,0:T(8,128)(2,1)} async-done(((bf16[2048,1024]{1,0:T(8,128)(2,1)}), bf16[256,1024]{1,0:T(8,128)(2,1)}) %reduce-scatter.16.cloned.1.call-update) | async-done | bytes 524304 | tf_op jit(solution)/shard_map/reduce_scatter | solution.py:254
  504.6 36.7 %all-gather.17.cloned.1.call-done = bf16[2048,1024]{1,0:T(8,128)(2,1)} async-done(((bf16[256,1024]{1,0:T(8,128)(2,1)}), bf16[2048,1024]{1,0:T(8,128)(2,1)}) %all-gather.17.cloned.1.call-update) | async-done | bytes 4194320 | tf_op jit(solution)/shard_map/all_gather | solution.py:250
  541.3 6.9 multiply_convert_fusion.1
  554.2 51.1 %reduce-scatter.18.cloned.1.call-done = bf16[256,1024]{1,0:T(8,128)(2,1)} async-done(((bf16[2048,1024]{1,0:T(8,128)(2,1)}), bf16[256,1024]{1,0:T(8,128)(2,1)}) %reduce-scatter.18.cloned.1.call-update) | async-done | bytes 524304 | tf_op jit(solution)/shard_map/reduce_scatter | solution.py:254
  610.1 36.6 %all-gather.19.cloned.1.call-done = bf16[2048,1024]{1,0:T(8,128)(2,1)} async-done(((bf16[256,1024]{1,0:T(8,128)(2,1)}), bf16[2048,1024]{1,0:T(8,128)(2,1)}) %all-gather.19.cloned.1.call-update) | async-done | bytes 4194320 | tf_op jit(solution)/shard_map/all_gather | solution.py:250
  651.7 11.7 all-reduce.3
  679.7 48.5 %reduce-scatter.20.cloned.1.call-done = bf16[256,1024]{1,0:T(8,128)(2,1)} async-done(((bf16[2048,1024]{1,0:T(8,128)(2,1)}), bf16[256,1024]{1,0:T(8,128)(2,1)}) %reduce-scatter.20.cloned.1.call-update) | async-done | bytes 524304 | tf_op jit(solution)/shard_map/reduce_scatter | solution.py:254
  732.8 36.7 %all-gather.21.cloned.1.call-done = bf16[2048,1024]{1,0:T(8,128)(2,1)} async-done(((bf16[256,1024]{1,0:T(8,128)(2,1)}), bf16[2048,1024]{1,0:T(8,128)(2,1)}) %all-gather.21.cloned.1.call-update) | async-done | bytes 4194320 | tf_op jit(solution)/shard_map/all_gather | solution.py:250
  773.7 27.2 %attend_back.1 = (bf16[2048,384]{1,0:T(8,128)(2,1)}, f32[16,512]{1,0:T(8,128)}) custom-call(s32[8]{0:T(128)} %get-tuple-element.146.low_ref, s32[8]{0:T(128)} %get-tuple-element.145.high_ref, bf16[2048,384]{1,0:T(8,128)(2,1)} %convolution_convert_fusion.8.q_ref.k_ref.v_ref, bf16[2048,384]{1,0:T(8,128)(2,1)} %convolution_convert_fusion.8.q_ref.k_ref.v_ref, ...), custom_call_target="tpu_custom_call" | custom-call | tf_op jit(solution)/shard_map/attend_back/pallas_call | solution.py:224
  806.7 54.3 %reduce-scatter.22.cloned.1.call-done = bf16[256,1024]{1,0:T(8,128)(2,1)} async-done(((bf16[2048,1024]{1,0:T(8,128)(2,1)}), bf16[256,1024]{1,0:T(8,128)(2,1)}) %reduce-scatter.22.cloned.1.call-update) | async-done | bytes 524304 | tf_op jit(solution)/shard_map/reduce_scatter | solution.py:254
  865.7 36.3 %all-gather.23.cloned.1.call-done = bf16[2048,1024]{1,0:T(8,128)(2,1)} async-done(((bf16[256,1024]{1,0:T(8,128)(2,1)}), bf16[2048,1024]{1,0:T(8,128)(2,1)}) %all-gather.23.cloned.1.call-update) | async-done | bytes 4194320 | tf_op jit(solution)/shard_map/all_gather | solution.py:250
  901.9 7.1 multiply_convert_fusion
  927.8 7.0 convolution_convert_fusion.10
  934.8 12.0 all-to-all-done.7
  1032.7 11.9 reduce-scatter.26.cloned.1.call-done
  1044.6 12.6 all-reduce.2
  1057.7 205.9 %all-reduce.7.cloned.1.call-done = (bf16[128,4096]{0,1:T(8,128)(2,1)}, bf16[128,4096]{0,1:T(8,128)(2,1)}, bf16[512,1024]{1,0:T(8,128)(2,1)}, bf16[128,3072]{1,0:...) async-done(((bf16[128,4096]{0,1:T(8,128)(2,1)}, bf16[128,4096]{0,1:T(8,128)(2,1)}, ...) | async-done | bytes 6029328 | tf_op jit(solution)/shard_map/psum | solution.py:276
  (328 shorter events, 260.6 us)
Async XLA Ops:
  7.2 435.8 %copy-start = (bf16[512,1024]{1,0:T(8,128)(2,1)S(1)}, bf16[512,1024]{1,0:T(8,128)(2,1)}, u32[]{:S(2)}) copy-start(bf16[512,1024]{1,0:T(8,128)(2,1)} %param.42) | copy-start | bytes 3145732
  7.2 62.9 %all-gather.9.cloned.1.call-start = ((), (), s32[]{:S(2)}) async-start(), calls=%async_computation.17 | async-start | bytes 4718592 | tf_op jit(solution)/shard_map/all_gather | solution.py:250
  26.0 106.4 %reduce-scatter.10.cloned.1.call-start = ((), (), s32[]{:S(2)}) async-start(), calls=%async_computation.18 | async-start | bytes 4718592 | tf_op jit(solution)/shard_map/reduce_scatter | solution.py:254
  81.1 97.7 %all-gather.11.cloned.1.call-start = ((), (), s32[]{:S(2)}) async-start(), calls=%async_computation.19 | async-start | bytes 4718592 | tf_op jit(solution)/shard_map/all_gather | solution.py:250
  137.6 21.6 %all-to-all-start.1 = ((bf16[128,3,8,128]{0,3,1,2:T(8,128)(2,1)}), bf16[128,3,8,128]{0,3,1,2:T(8,128)(2,1)S(1)}, u32[]{:S(2)}, u32[]{:S(2)}) async-start(bf16[128,3,8,128]{0,3,1,2:T(8,128)(2,1)} %copy.121), calls=%async_computation.2 | async-start | bytes 1572864 | tf_op jit(solution)/shard_map/all_to_all | solution.py:263
  141.2 118.8 %reduce-scatter.12.cloned.1.call-start = ((), (), s32[]{:S(2)}) async-start(), calls=%async_computation.20 | async-start | bytes 4718592 | tf_op jit(solution)/shard_map/reduce_scatter | solution.py:254
  206.1 57.1 %copy-start.37 = (bf16[128,2048]{1,0:T(8,128)(2,1)S(1)}, bf16[128,2048]{1,0:T(8,128)(2,1)}, u32[]{:S(2)}) copy-start(bf16[128,2048]{1,0:T(8,128)(2,1)} %param.35) | copy-start | bytes 1572868
  206.2 61.8 %copy-start.61 = (bf16[128]{0:T(256)(128)(2,1)S(1)}, bf16[128]{0:T(256)(128)(2,1)}, u32[]{:S(2)}) copy-start(bf16[128]{0:T(256)(128)(2,1)} %param.38) | copy-start | bytes 772
  206.2 62.3 %copy-start.57 = (bf16[128]{0:T(256)(128)(2,1)S(1)}, bf16[128]{0:T(256)(128)(2,1)}, u32[]{:S(2)}) copy-start(bf16[128]{0:T(256)(128)(2,1)} %param.37) | copy-start | bytes 772
  206.2 62.8 %copy-start.56 = (bf16[5,128]{1,0:T(8,128)(2,1)S(1)}, bf16[5,128]{1,0:T(8,128)(2,1)}, u32[]{:S(2)}) copy-start(bf16[5,128]{1,0:T(8,128)(2,1)} %param.36) | copy-start | bytes 3844
  206.2 62.8 %copy-start.40 = (s32[2048]{0:T(1024)S(1)}, s32[2048]{0:T(1024)}, u32[]{:S(2)}) copy-start(s32[2048]{0:T(1024)} %copy-done.39) | copy-start | bytes 24580
  206.2 62.8 %copy-start.42 = (s32[2048]{0:T(1024)S(1)}, s32[2048]{0:T(1024)}, u32[]{:S(2)}) copy-start(s32[2048]{0:T(1024)} %copy-done.41) | copy-start | bytes 24580
  206.2 96.6 %all-gather.13.cloned.1.call-start = ((), (), s32[]{:S(2)}) async-start(), calls=%async_computation.21 | async-start | bytes 4718592 | tf_op jit(solution)/shard_map/all_gather | solution.py:250
  264.4 16.7 %all-to-all-start.2 = ((bf16[128,2,8,128]{0,3,1,2:T(8,128)(2,1)}), bf16[128,2,8,128]{0,3,1,2:T(8,128)(2,1)S(1)}, u32[]{:S(2)}, u32[]{:S(2)}) async-start(bf16[128,2,8,128]{0,3,1,2:T(8,128)(2,1)} %copy.124), calls=%async_computation.4 | async-start | bytes 1048576 | tf_op jit(solution)/shard_map/all_to_all | solution.py:263
  267.9 118.0 %reduce-scatter.14.cloned.1.call-start = ((), (), s32[]{:S(2)}) async-start(), calls=%async_computation.22 | async-start | bytes 4718592 | tf_op jit(solution)/shard_map/reduce_scatter | solution.py:254
  335.9 100.2 %all-gather.15.cloned.1.call-start = ((), (), s32[]{:S(2)}) async-start(), calls=%async_computation.23 | async-start | bytes 4718592 | tf_op jit(solution)/shard_map/all_gather | solution.py:250
  388.7 110.0 %reduce-scatter.16.cloned.1.call-start = ((), (), s32[]{:S(2)}) async-start(), calls=%async_computation.24 | async-start | bytes 4718592 | tf_op jit(solution)/shard_map/reduce_scatter | solution.py:254
  447.4 93.9 %all-gather.17.cloned.1.call-start = ((), (), s32[]{:S(2)}) async-start(), calls=%async_computation.25 | async-start | bytes 4718592 | tf_op jit(solution)/shard_map/all_gather | solution.py:250
  504.6 100.6 %reduce-scatter.18.cloned.1.call-start = ((), (), s32[]{:S(2)}) async-start(), calls=%async_computation.26 | async-start | bytes 4718592 | tf_op jit(solution)/shard_map/reduce_scatter | solution.py:254
  553.9 92.8 %all-gather.19.cloned.1.call-start = ((), (), s32[]{:S(2)}) async-start(), calls=%async_computation.27 | async-start | bytes 4718592 | tf_op jit(solution)/shard_map/all_gather | solution.py:250
  610.0 118.2 %reduce-scatter.20.cloned.1.call-start = ((), (), s32[]{:S(2)}) async-start(), calls=%async_computation.28 | async-start | bytes 4718592 | tf_op jit(solution)/shard_map/reduce_scatter | solution.py:254
  679.7 89.8 %all-gather.21.cloned.1.call-start = ((), (), s32[]{:S(2)}) async-start(), calls=%async_computation.29 | async-start | bytes 4718592 | tf_op jit(solution)/shard_map/all_gather | solution.py:250
  732.7 128.3 %reduce-scatter.22.cloned.1.call-start = ((), (), s32[]{:S(2)}) async-start(), calls=%async_computation.30 | async-start | bytes 4718592 | tf_op jit(solution)/shard_map/reduce_scatter | solution.py:254
  806.6 56.0 %copy-start.20 = (f32[256,1024]{1,0:T(8,128)S(1)}, f32[256,1024]{1,0:T(8,128)}, u32[]{:S(2)}) copy-start(f32[256,1024]{1,0:T(8,128)} %get-tuple-element.106) | copy-start | bytes 3145732
  806.6 95.3 %all-gather.23.cloned.1.call-start = ((), (), s32[]{:S(2)}) async-start(), calls=%async_computation.31 | async-start | bytes 4718592 | tf_op jit(solution)/shard_map/all_gather | solution.py:250
  865.2 143.2 %reduce-scatter.24.cloned.1.call-start = ((), (), s32[]{:S(2)}) async-start(), calls=%async_computation.32 | async-start | bytes 4718592 | tf_op jit(solution)/shard_map/reduce_scatter | solution.py:254
  923.5 23.2 %all-to-all-start.7 = ((bf16[8,2,32768]{2,1,0:T(2,128)(2,1)}), bf16[8,2,32768]{2,1,0:T(2,128)(2,1)}, u32[]{:S(2)}, u32[]{:S(2)}) async-start(bf16[8,2,32768]{2,1,0:T(2,128)(2,1)} %reshape.446), calls=%async_computation.16 | async-start | bytes 2097152 | tf_op jit(solution)/shard_map/all_to_all | solution.py:271
  959.5 14.9 %all-to-all-start.6 = ((bf16[1024,2,1,128]{3,1,2,0:T(2,128)(2,1)}), bf16[1024,2,1,128]{3,1,2,0:T(2,128)(2,1)S(1)}, u32[]{:S(2)}, u32[]{:S(2)}) async-start(bf16[1024,2,1,128]{3,1,2,0:T(2,128)(2,1)} %copy.133), calls=%async_computation.15 | async-start | bytes 1048576 | tf_op jit(solution)/shard_map/all_to_all | solution.py:271
  975.2 19.0 %all-to-all-start.5 = ((bf16[1024,3,1,128]{3,1,2,0:T(4,128)(2,1)}), bf16[1024,3,1,128]{3,1,2,0:T(4,128)(2,1)S(1)}, u32[]{:S(2)}, u32[]{:S(2)}) async-start(bf16[1024,3,1,128]{3,1,2,0:T(4,128)(2,1)} %copy.131), calls=%async_computation.14 | async-start | bytes 2097152 | tf_op jit(solution)/shard_map/all_to_all | solution.py:271
  1004.8 18.9 %all-to-all-start.4 = ((bf16[8,2,32768]{2,1,0:T(2,128)(2,1)}), bf16[8,2,32768]{2,1,0:T(2,128)(2,1)S(1)}, u32[]{:S(2)}, u32[]{:S(2)}) async-start(bf16[8,2,32768]{2,1,0:T(2,128)(2,1)} %reshape.444), calls=%async_computation.13 | async-start | bytes 2097152 | tf_op jit(solution)/shard_map/all_to_all | solution.py:271
  1008.4 36.3 %reduce-scatter.26.cloned.1.call-start = ((), (), s32[]{:S(2)}) async-start(), calls=%async_computation.33 | async-start | bytes 36864 | tf_op jit(solution)/shard_map/reduce_scatter | solution.py:430
  1010.9 252.8 %all-reduce.7.cloned.1.call-start = ((), (), s32[]{:S(2)}) async-start(), calls=%async_computation.34 | async-start | bytes 12058624 | tf_op jit(solution)/shard_map/psum | solution.py:276
  (64 other events, 1044.5 us)
Sparse Core Ops, SparseCore 0:
  26.1 43.9 all-gather.8
  81.3 51.1 reduce-scatter.9
  135.3 43.5 all-gather.10
  206.3 53.7 reduce-scatter.11
  263.4 39.3 all-gather.12
  336.0 49.7 reduce-scatter.13
  388.8 47.2 all-gather.14
  447.5 51.1 reduce-scatter.15
  504.7 36.5 all-gather.16
  554.1 51.1 reduce-scatter.17
  610.1 36.5 all-gather.18
  679.8 48.3 reduce-scatter.19
  732.8 36.5 all-gather.20
  806.7 54.2 reduce-scatter.21
  865.3 36.5 all-gather.22
  914.9 56.0 reduce-scatter.23
  1011.9 32.7 reduce-scatter.25
  1049.1 214.5 all-reduce.6
